TPU v7x, 8 devices: a whole 2x2x1 slice. The times are simulated.
8 devices in a mesh: depth: 2 (over z, y), col: 2 (over x), row: 2 (over core).
Axes of the slice: x: 2, y: 2, z: 1, core: 2. Of those that a mesh axis runs over, the one named last changes fastest.
Arguments:
- x: bfloat16 [32, 512, 4096], P(('depth', 'row'), None, 'col')
- ln_scale: float32 [4096], P('col')
- ln_bias: float32 [4096], P('col')
- w_qkv: bfloat16 [4096, 12288], P('row', 'col')
- b_qkv: float32 [32, 384], P('col')
- w_out: bfloat16 [4096, 4096], P('row', 'col')
- b_out: float32 [4096], P('col')
- grad_y: bfloat16 [32, 512, 4096], P(('depth', 'row'), None, 'col')
Outputs:
- output 1: bfloat16 [32, 512, 4096], P(('depth', 'row'), None, 'col')
- output 2: bfloat16 [32, 512, 4096], P(('depth', 'row'), None, 'col')
- output 3: float32 [4096, 12288], P('row', 'col')
- output 4: float32 [32, 384], P('col')
- output 5: float32 [4096, 4096], P('row', 'col')
- output 6: float32 [4096], P('col')
- output 7: float32 [4096], P('col')
- output 8: float32 [4096], P('col')
All inputs are finite; a program needn't handle non-finite values.
Results may differ from a plain program's by a relative error of at most 0.00731328.
Values are sent between devices in bfloat16 or wider.
A program may use at most 1 GiB of HBM per device.

v0:
```python
import jax
import jax.numpy as jnp
from jax import lax
from jax.sharding import PartitionSpec as P


def solution(mesh):
    col_size = mesh.shape['col']
    act_spec = P(('depth', 'row'), None, 'col')
    vec_spec = P('col')
    mat_spec = P('row', 'col')
    head_vec_spec = P('col', None)

    def block_fn(x, ln_scale, ln_bias, w_qkv, b_qkv, w_out, b_out, grad_y):
        batch_loc, seq_len, d_loc = x.shape
        d_model = d_loc * col_size
        heads_loc, three_dh = b_qkv.shape
        head_dim = three_dh // 3
        attn_scale = head_dim ** -0.5
        x_f32 = x.astype(jnp.float32)
        mean_x = lax.psum(jnp.sum(x_f32, axis=-1, keepdims=True), 'col') / d_model
        centered = x_f32 - mean_x
        var_x = lax.psum(jnp.sum(centered * centered, axis=-1, keepdims=True), 'col') / d_model
        inv_std = lax.rsqrt(var_x + 1e-5)
        x_hat = centered * inv_std
        h_loc = (x_hat * ln_scale + ln_bias).astype(jnp.bfloat16)
        h_full = lax.all_gather(h_loc, 'col', axis=2, tiled=True)
        w_qkv_cols = lax.all_gather(w_qkv, 'row', axis=0, tiled=True)
        qkv_acc = jnp.einsum('bsk,km->bsm', h_full, w_qkv_cols, preferred_element_type=jnp.float32)
        qkv = (qkv_acc.reshape(batch_loc, seq_len, heads_loc, 3, head_dim) + b_qkv.reshape(heads_loc, 3, head_dim)).astype(jnp.bfloat16)
        q_heads = qkv[:, :, :, 0]
        k_heads = qkv[:, :, :, 1]
        v_heads = qkv[:, :, :, 2]
        causal = lax.broadcasted_iota(jnp.int32, (seq_len, seq_len), 0) >= lax.broadcasted_iota(jnp.int32, (seq_len, seq_len), 1)
        scores = jnp.einsum('bqhe,bkhe->bhqk', q_heads, k_heads, preferred_element_type=jnp.float32) * attn_scale
        attn_prob = jax.nn.softmax(jnp.where(causal, scores, -1e30), axis=-1)
        prob_b = attn_prob.astype(jnp.bfloat16)
        attn_out = jnp.einsum('bhqk,bkhe->bqhe', prob_b, v_heads, preferred_element_type=jnp.float32).astype(jnp.bfloat16)
        o_full = lax.all_gather(attn_out.reshape(batch_loc, seq_len, d_loc), 'col', axis=2, tiled=True)
        w_out_cols = lax.all_gather(w_out, 'row', axis=0, tiled=True)
        projected = jnp.einsum('bsk,km->bsm', o_full, w_out_cols, preferred_element_type=jnp.float32)
        y_out = (x_f32 + projected + b_out).astype(jnp.bfloat16)
        d_b_out = lax.psum(jnp.sum(grad_y, axis=(0, 1), dtype=jnp.float32), ('depth', 'row'))
        w_out_part = jnp.einsum('bsk,bsm->km', o_full, grad_y, preferred_element_type=jnp.float32)
        d_w_out = lax.psum(lax.psum_scatter(w_out_part, 'row', scatter_dimension=0, tiled=True), 'depth')
        d_out_part = jnp.einsum('bsm,km->bsk', grad_y, w_out_cols, preferred_element_type=jnp.float32)
        d_out = lax.psum_scatter(d_out_part, 'col', scatter_dimension=2, tiled=True).astype(jnp.bfloat16)
        d_out_heads = d_out.reshape(batch_loc, seq_len, heads_loc, head_dim)
        d_prob = jnp.einsum('bqhe,bkhe->bhqk', d_out_heads, v_heads, preferred_element_type=jnp.float32)
        d_v = jnp.einsum('bhqk,bqhe->bkhe', prob_b, d_out_heads, preferred_element_type=jnp.float32)
        row_dot = jnp.sum(attn_prob * d_prob, axis=-1, keepdims=True)
        d_scores = (attn_prob * (d_prob - row_dot) * attn_scale).astype(jnp.bfloat16)
        d_q = jnp.einsum('bhqk,bkhe->bqhe', d_scores, k_heads, preferred_element_type=jnp.float32)
        d_k = jnp.einsum('bhqk,bqhe->bkhe', d_scores, q_heads, preferred_element_type=jnp.float32)
        d_qkv = jnp.stack([d_q, d_k, d_v], axis=3).astype(jnp.bfloat16).reshape(batch_loc, seq_len, 3 * d_loc)
        d_b_qkv = lax.psum(jnp.sum(d_qkv, axis=(0, 1), dtype=jnp.float32).reshape(heads_loc, three_dh), ('depth', 'row'))
        w_qkv_part = jnp.einsum('bsk,bsm->km', h_full, d_qkv, preferred_element_type=jnp.float32)
        d_w_qkv = lax.psum(lax.psum_scatter(w_qkv_part, 'row', scatter_dimension=0, tiled=True), 'depth')
        d_h_part = jnp.einsum('bsm,km->bsk', d_qkv, w_qkv_cols, preferred_element_type=jnp.float32)
        d_h = lax.psum_scatter(d_h_part, 'col', scatter_dimension=2, tiled=True)
        d_ln_scale = lax.psum(jnp.sum(d_h * x_hat, axis=(0, 1)), ('depth', 'row'))
        d_ln_bias = lax.psum(jnp.sum(d_h, axis=(0, 1)), ('depth', 'row'))
        g_hat = d_h * ln_scale
        mean_g = lax.psum(jnp.sum(g_hat, axis=-1, keepdims=True), 'col') / d_model
        mean_gx = lax.psum(jnp.sum(g_hat * x_hat, axis=-1, keepdims=True), 'col') / d_model
        d_x = (grad_y.astype(jnp.float32) + inv_std * (g_hat - mean_g - x_hat * mean_gx)).astype(jnp.bfloat16)
        return y_out, d_x, d_w_qkv, d_b_qkv, d_w_out, d_b_out, d_ln_scale, d_ln_bias

    return jax.shard_map(block_fn, mesh=mesh, in_specs=(act_spec, vec_spec, vec_spec, mat_spec, head_vec_spec, mat_spec, vec_spec, act_spec), out_specs=(act_spec, act_spec, mat_spec, head_vec_spec, mat_spec, vec_spec, vec_spec, vec_spec), check_vma=False)
```

profile of v0, /device:TPU:0, one launch (start us, length us, event | category | flops | bytes accessed | tf_op | source)
XLA Modules:
  0.0 5499.5 jit_solution(13843881378003712045)
XLA Ops:
  39.4 16.5 fusion.26
  59.3 383.6 %all-gather.5.cloned.1.call-done = bf16[8,512,4096]{2,1,0:T(8,128)(2,1)} async-done(((bf16[8,512,2048]{2,1,0:T(8,128)(2,1)}), bf16[8,512,4096]{2,1,0:T(8,128)(2,1)}) %all-gather.5.cloned.1.call-update) | async-done | bytes 33554448 | tf_op jit(solution)/shard_map/all_gather | solution.py:27
  442.9 70.7 %all-gather.7.cloned.1.call-done = bf16[4096,6144]{1,0:T(8,128)(2,1)} async-done(((bf16[2048,6144]{1,0:T(8,128)(2,1)}), bf16[4096,6144]{1,0:T(8,128)(2,1)}) %all-gather.7.cloned.1.call-update) | async-done | bytes 50331664 | tf_op jit(solution)/shard_map/all_gather | solution.py:28
  513.6 232.2 %fusion.11 = f32[8,512,6144]{1,2,0:T(8,128)} fusion(bf16[8,512,4096]{2,1,0:T(8,128)(2,1)} %all-gather.5.cloned.1.call-done, bf16[4096,6144]{1,0:T(8,128)(2,1)} %all-gather.7.cloned.1.call-done), kind=kOutput, calls=%fused_computation.18 | convolution fusion | flops 206158430208 | bytes 184549376 | tf_op jit(solution)/shard_map/bsk,km->bsm/dot_general | solution.py:29
  745.9 97.0 %copy.50 = f32[8,512,16,3,128]{4,1,2,0,3:T(8,128)} copy(f32[8,512,16,3,128]{1,4,3,2,0:T(8,128)} %bitcast.5) | data formatting | bytes 201326592 | tf_op jit(solution)/shard_map/reshape | solution.py:30
  842.9 48.2 add_convert_fusion
  891.1 57.7 %fusion.43 = f32[8,16,512,512]{2,3,1,0:T(8,128)} fusion(bf16[8,512,16,3,128]{4,1,2,0,3:T(8,128)(2,1)} %add_convert_fusion), kind=kOutput, calls=%fused_computation.56 | convolution fusion | flops 8589934592 | bytes 167772160 | tf_op jit(solution)/shard_map/bqhe,bkhe->bhqk/dot_general | solution.py:35
  948.7 128.8 %fusion.62 = (f32[8,16,512]{2,1,0:T(8,128)S(1)}, f32[8,16,512,512]{2,3,1,0:T(8,128)}) fusion(f32[8,16,512,512]{2,3,1,0:T(8,128)} %fusion.43, pred[512,512]{0,1:T(8,128)(4,1)S(1)} %copy-done.6), kind=kOutput, calls=%fused_computation.74 | output fusion | flops 201327104 | bytes 268959744 | tf_op jit(solution)/shard_map/sub | solution.py:36
  1077.5 52.5 fusion.53
  1130.0 21.5 copy.53
  1151.6 79.1 %fusion.39 = f32[8,512,4096]{2,1,0:T(8,128)} fusion(bf16[8,512,2048]{2,1,0:T(8,128)(2,1)} %param.15, bf16[4096,2048]{1,0:T(8,128)(2,1)} %all-gather.11.cloned.1.call-done), kind=kOutput, calls=%fused_computation.52 | convolution fusion | flops 68719476736 | bytes 100663296 | tf_op jit(solution)/shard_map/bsm,km->bsk/dot_general | solution.py:46
  1230.8 307.6 %all-gather.9.cloned.1.call-done = bf16[8,512,4096]{2,1,0:T(8,128)(2,1)} async-done(((bf16[8,512,2048]{2,1,0:T(8,128)(2,1)}), bf16[8,512,4096]{2,1,0:T(8,128)(2,1)}) %all-gather.9.cloned.1.call-update) | async-done | bytes 33554448 | tf_op jit(solution)/shard_map/all_gather | solution.py:39
  1538.3 79.6 %convolution_bitcast_fusion.1 = f32[4096,2048]{1,0:T(8,128)} fusion(bf16[8,512,4096]{2,1,0:T(8,128)(2,1)} %all-gather.9.cloned.1.call-done, bf16[8,512,2048]{2,1,0:T(8,128)(2,1)} %param.15), kind=kOutput, calls=%fused_computation.48 | convolution fusion | flops 68719476736 | bytes 83886080 | tf_op jit(solution)/shard_map/bsk,bsm->km/dot_general | solution.py:44
  1618.0 648.1 %reduce-scatter.8.cloned.1.call-done = f32[8,512,2048]{2,1,0:T(8,128)} async-done(((f32[8,512,4096]{2,1,0:T(8,128)}), f32[8,512,2048]{2,1,0:T(8,128)}) %reduce-scatter.8.cloned.1.call-update) | async-done | bytes 33554448 | tf_op jit(solution)/shard_map/reduce_scatter | solution.py:47
  2266.1 17.9 convert_element_type.54
  2284.0 21.5 copy.79
  2305.6 55.3 %fusion.42 = f32[8,16,512,512]{2,3,1,0:T(8,128)} fusion(bf16[8,512,16,128]{1,3,2,0:T(8,128)(2,1)} %bitcast.103, bf16[8,512,16,3,128]{4,1,2,0,3:T(8,128)(2,1)} %add_convert_fusion), kind=kOutput, calls=%fused_computation.55 | convolution fusion | flops 8589934592 | bytes 167772160 | tf_op jit(solution)/shard_map/bqhe,bkhe->bhqk/dot_general | solution.py:49
  2360.8 169.3 %fusion.47 = bf16[8,512,16,1,128]{1,4,2,0,3:T(8,128)(2,1)} fusion(f32[8,16,512,512]{2,3,1,0:T(8,128)} %fusion.42, bf16[8,512,16,3,128]{4,1,2,0,3:T(8,128)(2,1)} %add_convert_fusion, f32[8,16,512,512]{2,3,1,0:T(8,128)} %get-tuple-element.25, f32[8,16,512]{2,1,0:T(8,128)S(1)} %copy-done.14), kind=kOutput, calls=%fused_computation.58 | convolution fusion | flops 8824881152 | bytes 570949632 | tf_op jit(solution)/shard_map/bhqk,bkhe->bqhe/dot_general | solution.py:53
  2530.1 169.7 %fusion.50 = bf16[8,512,16,1,128]{1,4,2,0,3:T(8,128)(2,1)} fusion(f32[8,16,512,512]{2,3,1,0:T(8,128)} %fusion.42, bf16[8,512,16,3,128]{4,1,2,0,3:T(8,128)(2,1)} %add_convert_fusion, f32[8,16,512,512]{2,3,1,0:T(8,128)} %get-tuple-element.25, f32[8,16,512]{2,1,0:T(8,128)S(1)} %copy-done.14), kind=kOutput, calls=%fused_computation.59 | convolution fusion | flops 8824881152 | bytes 570949632 | tf_op jit(solution)/shard_map/bhqk,bqhe->bkhe/dot_general | solution.py:54
  2699.8 53.1 fusion.44
  2752.9 34.0 convert_reduce_fusion
  2786.9 33.5 copy.61
  2820.4 221.1 %convolution_bitcast_fusion = f32[4096,6144]{1,0:T(8,128)} fusion(bf16[8,512,4096]{2,1,0:T(8,128)(2,1)} %all-gather.5.cloned.1.call-done, bf16[8,512,6144]{1,2,0:T(8,128)(2,1)} %bitcast.105), kind=kOutput, calls=%fused_computation.15 | convolution fusion | flops 206158430208 | bytes 184549376 | tf_op jit(solution)/shard_map/bsk,bsm->km/dot_general | solution.py:57
  3041.7 224.1 %fusion.9 = f32[8,512,4096]{2,1,0:T(8,128)} fusion(bf16[8,512,6144]{1,2,0:T(8,128)(2,1)} %bitcast.106, bf16[4096,6144]{1,0:T(8,128)(2,1)} %all-gather.7.cloned.1.call-done), kind=kOutput, calls=%fused_computation.16 | convolution fusion | flops 206158430208 | bytes 167772160 | tf_op jit(solution)/shard_map/bsm,km->bsk/dot_general | solution.py:59
  3266.6 80.1 %fusion.34 = bf16[8,512,2048]{2,1,0:T(8,128)(2,1)} fusion(bf16[8,512,2048]{2,1,0:T(8,128)(2,1)} %param.8, bf16[8,512,4096]{2,1,0:T(8,128)(2,1)} %all-gather.9.cloned.1.call-done, bf16[4096,2048]{1,0:T(8,128)(2,1)} %all-gather.11.cloned.1.call-done, f32[2048]{0:T(1024)S(1)} %copy-done.12), kind=kOutput, calls=%fused_computation.42 | convolution fusion | flops 68753031168 | bytes 83894272 | tf_op jit(solution)/shard_map/bsk,km->bsm/dot_general | solution.py:41
  3346.7 644.9 %reduce-scatter.10.cloned.1.call-done = f32[8,512,2048]{2,1,0:T(8,128)} async-done(((f32[8,512,4096]{2,1,0:T(8,128)}), f32[8,512,2048]{2,1,0:T(8,128)}) %reduce-scatter.10.cloned.1.call-update) | async-done | bytes 33554448 | tf_op jit(solution)/shard_map/reduce_scatter | solution.py:60
  3991.6 21.2 fusion.30
  4020.0 28.5 convert_reduce_fusion.2
  4048.5 12.9 all-reduce.1
  4061.4 1384.9 %all-reduce.6.cloned.1.call-done = (f32[2048,6144]{1,0:T(8,128)}, f32[2048,2048]{1,0:T(8,128)}) async-done(((f32[2048,6144]{1,0:T(8,128)}, f32[2048,2048]{1,0:T(8,128)}), (f32[2048,6144]{1,0:T(8,128)}, f32[2048,2048]{1,0:T(8,128)})) %all-reduce.6.cloned.1.call-update) | async-done | bytes 67108880 | tf_op jit(solution)/shard_map/psum | solution.py:58
  5446.3 34.5 copy.86
  5480.9 11.8 copy.87
  (62 shorter events, 43.9 us)
Async XLA Ops:
  7.2 51.6 copy-start
  7.2 32.2 copy-start.11
  7.2 32.2 copy-start.9
  7.2 435.7 %all-gather.5.cloned.1.call-start = ((), (), s32[]{:S(2)}) async-start(), calls=%async_computation.4 | async-start | bytes 50331648 | tf_op jit(solution)/shard_map/all_gather | solution.py:27
  24.2 31.7 copy-start.2
  38.8 0.6 copy-start.4
  55.9 457.7 %all-gather.7.cloned.1.call-start = ((), (), s32[]{:S(2)}) async-start(), calls=%async_computation.5 | async-start | bytes 75497472 | tf_op jit(solution)/shard_map/all_gather | solution.py:28
  56.6 1094.9 %all-gather.11.cloned.1.call-start = ((), (), s32[]{:S(2)}) async-start(), calls=%async_computation.7 | async-start | bytes 25165824 | tf_op jit(solution)/shard_map/all_gather | solution.py:40
  57.4 1481.0 %all-gather.9.cloned.1.call-start = ((), (), s32[]{:S(2)}) async-start(), calls=%async_computation.6 | async-start | bytes 50331648 | tf_op jit(solution)/shard_map/all_gather | solution.py:39
  745.9 97.0 %copy-start.8 = (f32[16,3,128]{2,0,1:T(8,128)S(1)}, f32[16,3,128]{2,0,1:T(8,128)}, u32[]{:S(2)}) copy-start(f32[16,3,128]{2,0,1:T(8,128)} %copy_bitcast_fusion.1) | copy-start | bytes 73732
  891.0 57.7 %copy-start.6 = (pred[512,512]{0,1:T(8,128)(4,1)S(1)}, pred[512,512]{0,1:T(8,128)(4,1)}, u32[]{:S(2)}) copy-start(pred[512,512]{0,1:T(8,128)(4,1)} %iota_compare_fusion) | copy-start | bytes 786436
  1077.5 52.5 copy-start.13
  1151.5 1114.6 %reduce-scatter.8.cloned.1.call-start = ((), (), s32[]{:S(2)}) async-start(), calls=%async_computation.8 | async-start | bytes 100663296 | tf_op jit(solution)/shard_map/reduce_scatter | solution.py:47
  1230.7 2035.1 %reduce-scatter.12.cloned.1.call-start = ((), (), s32[]{:S(2)}) async-start(), calls=%async_computation.10 | async-start | bytes 50331648 | tf_op jit(solution)/shard_map/reduce_scatter | solution.py:45
  1618.0 1647.9 %reduce-scatter.14.cloned.1.call-start = ((), (), s32[]{:S(2)}) async-start(), calls=%async_computation.11 | async-start | bytes 150994944
  2305.6 55.3 %copy-start.14 = (f32[8,16,512]{2,1,0:T(8,128)S(1)}, f32[8,16,512]{2,1,0:T(8,128)}, u32[]{:S(2)}) copy-start(f32[8,16,512]{2,1,0:T(8,128)} %copy-done.13) | copy-start | bytes 786436
  3041.6 949.9 %reduce-scatter.10.cloned.1.call-start = ((), (), s32[]{:S(2)}) async-start(), calls=%async_computation.9 | async-start | bytes 100663296 | tf_op jit(solution)/shard_map/reduce_scatter | solution.py:60
  3265.8 2180.6 %all-reduce.6.cloned.1.call-start = ((), (), s32[]{:S(2)}) async-start(), calls=%async_computation.12 | async-start | bytes 134217728 | tf_op jit(solution)/shard_map/psum | solution.py:58
  3265.9 0.7 copy-start.12
  3266.6 80.1 %copy-start.7 = (f32[16,3,128]{2,0,1:T(8,128)S(1)}, f32[16,3,128]{2,0,1:T(8,128)}, u32[]{:S(2)}) copy-start(f32[16,3,128]{2,0,1:T(8,128)} %get-tuple-element.20) | copy-start | bytes 73732
  3266.6 725.0 %copy-start.3 = (f32[8,512]{1,0:T(8,128)S(1)}, f32[8,512]{1,0:T(8,128)}, u32[]{:S(2)}) copy-start(f32[8,512]{1,0:T(8,128)} %copy-done.2) | copy-start | bytes 49156
  3266.6 725.0 %copy-start.5 = (f32[8,512]{1,0:T(8,128)S(1)}, f32[8,512]{1,0:T(8,128)}, u32[]{:S(2)}) copy-start(f32[8,512]{1,0:T(8,128)} %copy-done.4) | copy-start | bytes 49156
  3266.6 725.0 %copy-start.10 = (f32[2048]{0:T(1024)S(1)}, f32[2048]{0:T(1024)}, u32[]{:S(2)}) copy-start(f32[2048]{0:T(1024)} %param.9) | copy-start | bytes 24580
  5446.3 46.3 copy-start.1
Sparse Core Ops, SparseCore 0:
  56.0 386.8 all-gather.4
  444.4 69.1 all-gather.6
  515.2 28.9 all-gather.10
  1151.6 386.6 all-gather.8
  1540.4 725.6 reduce-scatter.7
  2268.2 39.2 reduce-scatter.11
  3041.7 93.5 reduce-scatter.13
  3265.9 725.6 reduce-scatter.9
  3994.1 1452.2 all-reduce.5
where the time goes:
time: 5500 us
  waiting for transfers between devices  3440 us (63%)
  matrix products  1470 us (27%)
  other arithmetic  311 us (6%)
  local copies, waits for them, and re-layouts  221 us (4%)
    psum x1, waiting for transfers between devices, block_fn(): lax.psum(lax.psum_scatter(w_qkv_part, 'row', scatter_dimension=0, tiled=T...  1380 us
    reduce_scatter x1, waiting for transfers between devices, block_fn(): lax.psum_scatter(d_out_part, 'col', scatter_dimension=2, tiled=True)  648 us
    reduce_scatter x1, waiting for transfers between devices, block_fn(): d_h = lax.psum_scatter(d_h_part, 'col', scatter_dimension=2, tiled=True)  645 us
    all_gather x1, waiting for transfers between devices, block_fn(): h_full = lax.all_gather(h_loc, 'col', axis=2, tiled=True)  384 us
    all_gather x1, waiting for transfers between devices, block_fn(): lax.all_gather(attn_out.reshape(batch_loc, seq_len, d_loc), 'col', axis=2...  308 us
    dot_general x1, matrix products, block_fn(): jnp.einsum('bsk,km->bsm', h_full, w_qkv_cols, preferred_element_type=jnp....  232 us
    dot_general x1, matrix products, block_fn(): jnp.einsum('bsm,km->bsk', d_qkv, w_qkv_cols, preferred_element_type=jnp.f...  224 us
    dot_general x1, matrix products, block_fn(): jnp.einsum('bsk,bsm->km', h_full, d_qkv, preferred_element_type=jnp.float32)  221 us
  transfers between devices with their start and end apart: 9, of which 6 were waited for; matrix products, arithmetic and copies ran while one was open for 35% of the time, Pallas kernels for 0%

commit v1 on v0

v1 whole, which is shorter than its diff:
```python
import functools

import jax
import jax.numpy as jnp
from jax import lax
from jax.experimental import pallas as pl
from jax.experimental.pallas import tpu as pltpu
from jax.sharding import PartitionSpec as P


F32 = jnp.float32
BF16 = jnp.bfloat16
NEG = -1e30
LOG2E = 1.4426950408889634
DEP, COL, ROW = "depth", "col", "row"
SWAP = ((0, 1), (1, 0))


def nt(a, b):
    return lax.dot_general(a, b, (((1,), (1,)), ((), ())), preferred_element_type=F32)


def tn(a, b):
    return lax.dot_general(a, b, (((0,), (0,)), ((), ())), preferred_element_type=F32)


def nn(a, b):
    return lax.dot_general(a, b, (((1,), (0,)), ((), ())), preferred_element_type=F32)


def ln_kernel(d_model, flag_ref, xo_ref, xp_ref, so_ref, bo_ref, sp_ref, bp_ref, *refs):
    h_ref, ha_ref, hb_ref, m_ref, r_ref = refs[-5:]
    half = xo_ref.shape[1]
    xo = xo_ref[...].astype(F32)
    xp = xp_ref[...].astype(F32)
    mean = (jnp.sum(xo, -1, keepdims=True) + jnp.sum(xp, -1, keepdims=True)) / d_model
    co = xo - mean
    cp = xp - mean
    var = (jnp.sum(co * co, -1, keepdims=True) + jnp.sum(cp * cp, -1, keepdims=True)) / d_model
    inv = lax.rsqrt(var + 1e-5)
    m_ref[...] = mean
    r_ref[...] = inv
    ho = (co * inv * so_ref[...] + bo_ref[...]).astype(BF16)
    hp = (cp * inv * sp_ref[...] + bp_ref[...]).astype(BF16)
    flag = flag_ref[0]

    @pl.when(flag == 1)
    def _():
        ha_ref[...] = ho
        hb_ref[...] = hp
        h_ref[:, :half] = ho
        h_ref[:, half:] = hp

    @pl.when(flag == 0)
    def _():
        ha_ref[...] = hp
        hb_ref[...] = ho
        h_ref[:, :half] = hp
        h_ref[:, half:] = ho


def layer_norm(flag, x_own, x_oth, vecs, carry, base, total):
    rows, half = x_own.shape
    blk = 256
    b0 = base // blk
    row_spec = pl.BlockSpec((blk, half), lambda i, f: (i, 0))
    vec_spec = pl.BlockSpec((1, half), lambda i, f: (0, 0))
    any_spec = pl.BlockSpec(memory_space=pl.ANY)
    n_carry = 0 if carry is None else 2
    return pl.pallas_call(
        functools.partial(ln_kernel, 2 * half),
        out_shape=(
            jax.ShapeDtypeStruct((rows, 2 * half), BF16),
            jax.ShapeDtypeStruct((total, half), BF16),
            jax.ShapeDtypeStruct((total, half), BF16),
            jax.ShapeDtypeStruct((rows, 1), F32),
            jax.ShapeDtypeStruct((rows, 1), F32),
        ),
        grid_spec=pltpu.PrefetchScalarGridSpec(
            num_scalar_prefetch=1,
            grid=(rows // blk,),
            in_specs=[row_spec, row_spec, vec_spec, vec_spec, vec_spec, vec_spec] + [any_spec] * n_carry,
            out_specs=(
                pl.BlockSpec((blk, 2 * half), lambda i, f: (i, 0)),
                pl.BlockSpec((blk, half), lambda i, f: (b0 + i, 0)),
                pl.BlockSpec((blk, half), lambda i, f: (b0 + i, 0)),
                pl.BlockSpec((blk, 1), lambda i, f: (i, 0)),
                pl.BlockSpec((blk, 1), lambda i, f: (i, 0)),
            ),
        ),
        input_output_aliases={} if carry is None else {7: 1, 8: 2},
        compiler_params=pltpu.CompilerParams(vmem_limit_bytes=48 * 2**20),
        cost_estimate=pl.CostEstimate(flops=rows * half * 2 * 40, bytes_accessed=rows * half * 12, transcendentals=0),
        name="layer_norm",
    )(flag, x_own, x_oth, *vecs, *(() if carry is None else carry))


def attn_fwd_kernel(heads, hd, qkv_ref, *refs):
    oi_ref, oa_ref = refs[-2:]
    seq = qkv_ref.shape[0]
    blk = 256
    scale = hd ** -0.5
    keep = lax.broadcasted_iota(jnp.int32, (blk, blk), 0) >= lax.broadcasted_iota(jnp.int32, (blk, blk), 1)
    for h in range(heads):
        c = h * 3 * hd
        for qb in range(seq // blk):
            q0 = qb * blk
            q = qkv_ref[q0 : q0 + blk, c : c + hd]
            s_d = jnp.where(keep, nt(q, qkv_ref[q0 : q0 + blk, c + hd : c + 2 * hd]), NEG)
            m = jnp.max(s_d, -1, keepdims=True)
            if qb:
                s_u = nt(q, qkv_ref[:q0, c + hd : c + 2 * hd])
                m = jnp.maximum(m, jnp.max(s_u, -1, keepdims=True))
            p_d = jnp.exp2((s_d - m) * (scale * LOG2E))
            den = jnp.sum(p_d, -1, keepdims=True)
            if qb:
                p_u = jnp.exp2((s_u - m) * (scale * LOG2E))
                den = den + jnp.sum(p_u, -1, keepdims=True)
            inv = 1.0 / den
            o = nn((p_d * inv).astype(BF16), qkv_ref[q0 : q0 + blk, c + 2 * hd : c + 3 * hd])
            if qb:
                o = o + nn((p_u * inv).astype(BF16), qkv_ref[:q0, c + 2 * hd : c + 3 * hd])
            o = o.astype(BF16)
            oi_ref[q0 : q0 + blk, h * hd : (h + 1) * hd] = o
            oa_ref[q0 : q0 + blk, h * hd : (h + 1) * hd] = o


def attn_fwd(qkv, hd, carry, base, total, seq):
    rows, width = qkv.shape
    n_heads = width // (3 * hd)
    hb = 4
    s0 = base // seq
    any_spec = pl.BlockSpec(memory_space=pl.ANY)
    n_carry = 0 if carry is None else 1
    n_seq = rows // seq
    return pl.pallas_call(
        functools.partial(attn_fwd_kernel, hb, hd),
        out_shape=(
            jax.ShapeDtypeStruct((rows, width // 3), BF16),
            jax.ShapeDtypeStruct((total, width // 3), BF16),
        ),
        grid=(n_seq, n_heads // hb),
        in_specs=[pl.BlockSpec((seq, 3 * hd * hb), lambda s, h: (s, h))] + [any_spec] * n_carry,
        out_specs=(
            pl.BlockSpec((seq, hd * hb), lambda s, h: (s, h)),
            pl.BlockSpec((seq, hd * hb), lambda s, h: (s0 + s, h)),
        ),
        input_output_aliases={} if carry is None else {1: 1},
        compiler_params=pltpu.CompilerParams(vmem_limit_bytes=48 * 2**20),
        cost_estimate=pl.CostEstimate(
            flops=n_seq * n_heads * 4 * seq * seq * hd * 2, bytes_accessed=rows * width * 4, transcendentals=n_seq * n_heads * seq * seq
        ),
        name="attn_fwd",
    )(qkv, *(() if carry is None else (carry,)))


def attn_bwd_kernel(heads, hd, qkv_ref, do_ref, *refs):
    dqkv_ref, tok_ref, dk_acc, dv_acc = refs[-4:]
    tok_ref[...] = jnp.zeros_like(tok_ref)
    seq = qkv_ref.shape[0]
    blk = 256
    scale = hd ** -0.5
    keep = lax.broadcasted_iota(jnp.int32, (blk, blk), 0) <= lax.broadcasted_iota(jnp.int32, (blk, blk), 1)
    for h in range(heads):
        c = h * 3 * hd
        for qb in reversed(range(seq // blk)):
            q0 = qb * blk
            q = qkv_ref[q0 : q0 + blk, c : c + hd]
            do = do_ref[q0 : q0 + blk, h * hd : (h + 1) * hd]
            spans = [(q0, blk, True)] + ([(0, q0, False)] if qb else [])
            s_list = []
            m = None
            for k0, kn, diag in spans:
                s = nt(qkv_ref[k0 : k0 + kn, c + hd : c + 2 * hd], q)
                if diag:
                    s = jnp.where(keep, s, NEG)
                s_list.append(s)
                mm = jnp.max(s, 0, keepdims=True)
                m = mm if m is None else jnp.maximum(m, mm)
            e_list = [jnp.exp2((s - m) * (scale * LOG2E)) for s in s_list]
            den = functools.reduce(lambda a, b: a + b, [jnp.sum(e, 0, keepdims=True) for e in e_list])
            inv = 1.0 / den
            p_list = [e * inv for e in e_list]
            dp_list = [nt(qkv_ref[k0 : k0 + kn, c + 2 * hd : c + 3 * hd], do) for k0, kn, _ in spans]
            dot = functools.reduce(lambda a, b: a + b, [jnp.sum(p * dp, 0, keepdims=True) for p, dp in zip(p_list, dp_list)])
            dq = None
            for (k0, kn, diag), p, dp in zip(spans, p_list, dp_list):
                ds = (p * (dp - dot) * scale).astype(BF16)
                dv = nn(p.astype(BF16), do)
                dk = nn(ds, q)
                part = tn(qkv_ref[k0 : k0 + kn, c + hd : c + 2 * hd], ds)
                dq = part if dq is None else dq + part
                if q0 + blk < seq:
                    dk = dk + dk_acc[k0 : k0 + kn, :]
                    dv = dv + dv_acc[k0 : k0 + kn, :]
                if diag:
                    dqkv_ref[k0 : k0 + kn, c + hd : c + 2 * hd] = dk.astype(BF16)
                    dqkv_ref[k0 : k0 + kn, c + 2 * hd : c + 3 * hd] = dv.astype(BF16)
                else:
                    dk_acc[k0 : k0 + kn, :] = dk
                    dv_acc[k0 : k0 + kn, :] = dv
            dqkv_ref[q0 : q0 + blk, c : c + hd] = dq.T.astype(BF16)


def attn_bwd(qkv, do, hd, carry, base, total, seq):
    rows, width = qkv.shape
    n_heads = width // (3 * hd)
    hb = 4
    s0 = base // seq
    any_spec = pl.BlockSpec(memory_space=pl.ANY)
    n_carry = 0 if carry is None else 1
    n_seq = rows // seq
    return pl.pallas_call(
        functools.partial(attn_bwd_kernel, hb, hd),
        out_shape=(jax.ShapeDtypeStruct((total, width), BF16), jax.ShapeDtypeStruct((8, 128), F32)),
        grid=(n_seq, n_heads // hb),
        in_specs=[
            pl.BlockSpec((seq, 3 * hd * hb), lambda s, h: (s, h)),
            pl.BlockSpec((seq, hd * hb), lambda s, h: (s, h)),
        ]
        + [any_spec] * n_carry,
        out_specs=(
            pl.BlockSpec((seq, 3 * hd * hb), lambda s, h: (s0 + s, h)),
            pl.BlockSpec((8, 128), lambda s, h: (0, 0)),
        ),
        scratch_shapes=[pltpu.VMEM((seq, hd), F32), pltpu.VMEM((seq, hd), F32)],
        input_output_aliases={} if carry is None else {2: 0},
        compiler_params=pltpu.CompilerParams(vmem_limit_bytes=48 * 2**20),
        cost_estimate=pl.CostEstimate(
            flops=n_seq * n_heads * 10 * seq * seq * hd * 2, bytes_accessed=rows * width * 6, transcendentals=n_seq * n_heads * seq * seq
        ),
        name="attn_bwd",
    )(qkv, do, *(() if carry is None else (carry,)))


class Line:
    def __init__(self):
        self.last = None

    def __call__(self, *vals):
        if self.last is None:
            return vals
        return lax.optimization_barrier(tuple(vals) + (self.last,))[:-1]

    def mark(self, v):
        self.last = v


def solution(mesh):
    act_spec = P((DEP, ROW), None, COL)
    vec_spec = P(COL)
    mat_spec = P(ROW, COL)
    head_vec_spec = P(COL, None)

    def block_fn(x, ln_scale, ln_bias, w_qkv, b_qkv, w_out, b_out, grad_y):
        n_seq, seq, dl = x.shape
        tok = n_seq * seq
        d_model = 2 * dl
        heads, three_hd = b_qkv.shape
        hd = three_hd // 3
        wide = heads * three_hd
        depth = lax.axis_index(DEP)
        col = lax.axis_index(COL)
        row = lax.axis_index(ROW)
        same = row == col
        X = x.reshape(tok, dl)
        G = grad_y.reshape(tok, dl)

        sizes = [2, 2, 2, 1, 1] if n_seq == 8 else [1] * n_seq
        spans = []
        at = 0
        for n in sizes:
            spans.append((at * seq, n * seq))
            at += n
        nc = len(spans)
        line = Line()

        def over(axis, v):
            return lax.ppermute(v, axis, SWAP)

        vec_oth = over(COL, jnp.concatenate([ln_scale, ln_bias]))
        vecs = (ln_scale.reshape(1, dl), ln_bias.reshape(1, dl), vec_oth[:dl].reshape(1, dl), vec_oth[dl:].reshape(1, dl))
        xs = [lax.slice_in_dim(X, a, a + n, axis=0) for a, n in spans]
        xr = [over(COL, xs[i]) for i in range(nc)]
        gs = [lax.slice_in_dim(G, a, a + n, axis=0) for a, n in spans]
        gr = {}

        w_peer = over(ROW, w_qkv)
        wo_peer = over(ROW, w_out)
        wo_own = jnp.where(same, w_out, wo_peer)
        wo_oth = jnp.where(same, wo_peer, w_out)
        line.mark(wo_oth)
        quarter = dl // 4
        qi = 2 * depth + row
        qt = over(COL, lax.dynamic_slice_in_dim(wo_oth, qi * quarter, quarter, axis=0))
        (wqa, wqb) = line(w_qkv, w_peer)
        w_cat = jnp.concatenate([wqa, wqb], axis=0)
        line.mark(w_cat)

        flag = same.astype(jnp.int32).reshape(1)
        bq = b_qkv.reshape(1, wide)
        hc, o_all = None, None
        qkvs, outs, means, invs = [], [], [], []
        g_after = {0: (0, 1), 1: (2,), 2: (3, 4)}
        for i, (a, n) in enumerate(spans):
            (xi, xri) = line(xs[i], xr[i])
            h, ha, hb, mean, inv = layer_norm(flag, xi, xri, vecs, hc, a, tok)
            hc = (ha, hb)
            means.append(mean)
            invs.append(inv)
            qkv = (nn(h, w_cat) + bq).astype(BF16)
            o, o_all = attn_fwd(qkv, hd, o_all, a, tok, seq)
            line.mark(o)
            qkvs.append(qkv)
            outs.append(o)
            for k in g_after.get(i, ()):
                (gk,) = line(gs[k])
                gr[k] = over(COL, gk)
        h_keep, h_send = hc

        (qt,) = line(qt)
        qt_r = over(ROW, qt)

        jo = (COL, ROW)
        ja = (DEP, COL, ROW)
        (g_e,) = line(G)
        early = tn(o_all, g_e)
        line.mark(early)
        early_p = lax.ppermute(early, jo, ((1, 0), (2, 3)))
        (qt, qt_r) = line(qt, qt_r)
        pair = jnp.where(row == 0, jnp.concatenate([qt, qt_r]), jnp.concatenate([qt_r, qt]))
        pair_d = over(DEP, pair)
        wo_blk = jnp.where(depth == 0, jnp.concatenate([pair, pair_d]), jnp.concatenate([pair_d, pair]))
        line.mark(wo_blk)

        dqkv = None
        ors = {}
        o_after = {2: (0, 1), 3: (2,), 4: (3, 4)}
        for i, (a, n) in enumerate(spans):
            (gi, gri) = line(gs[i], gr[i])
            do = (nt(gi, wo_own) + nt(gri, wo_blk)).astype(BF16)
            dqkv, t = attn_bwd(qkvs[i], do, hd, dqkv, a, tok, seq)
            line.mark(t)
            if i == 0:
                (e1, e2) = line(early, early_p)
                early = e1 + e2
                line.mark(early)
                early_y = lax.ppermute(early, ja, ((0, 4), (4, 0), (3, 7), (7, 3)))
            for k in o_after.get(i, ()):
                (ok,) = line(outs[k])
                ors[k] = over(COL, ok)

        n_j = 6
        wj = wide // n_j
        parts, sums, ys = {}, {}, {}
        dh_own, dh_rec = {}, {}

        def send(j):
            (hs, dd) = line(h_send, dqkv)
            v = tn(hs, lax.slice_in_dim(dd, j * wj, (j + 1) * wj, axis=1))
            line.mark(v)
            parts[j] = over(ROW, v)

        def keep(j):
            (hk, dd, pj) = line(h_keep, dqkv, parts[j])
            v = tn(hk, lax.slice_in_dim(dd, j * wj, (j + 1) * wj, axis=1)) + pj
            line.mark(v)
            sums[j] = v
            ys[j] = over(DEP, v)

        def dho(i):
            a, n = spans[i]
            (dd, ww) = line(dqkv, w_oth)
            v = nt(lax.slice_in_dim(dd, a, a + n, axis=0), ww)
            line.mark(v)
            dh_rec[i] = over(COL, v)

        def dhk(i):
            a, n = spans[i]
            (dd, ww) = line(dqkv, w_own)
            v = nt(lax.slice_in_dim(dd, a, a + n, axis=0), ww)
            line.mark(v)
            dh_own[i] = v

        d_w_qkv = None

        def fin(j):
            nonlocal d_w_qkv
            if d_w_qkv is None:
                d_w_qkv = jnp.zeros((dl, wide), F32)
            (s, r) = line(sums[j], ys[j])
            v = s + r
            line.mark(v)
            d_w_qkv = lax.dynamic_update_slice(d_w_qkv, v, (0, j * wj))

        send(0)
        send(1)
        keep(0)
        (wa, wb) = line(w_qkv, w_peer)
        w_own = jnp.where(same, wa, wb)
        w_oth = jnp.where(same, wb, wa)
        line.mark(w_oth)
        send(2)
        keep(1)
        dho(0)
        send(3)
        keep(2)
        dho(1)
        send(4)
        keep(3)
        dho(2)
        send(5)
        keep(4)
        dho(3)
        keep(5)
        dho(4)
        for i in range(nc):
            dhk(i)
        (dd,) = line(dqkv)
        d_b_qkv = jnp.sum(dd.astype(F32), axis=0).reshape(heads, three_hd)
        line.mark(d_b_qkv)
        (gg,) = line(G)
        d_b_out = jnp.sum(gg.astype(F32), axis=0)
        line.mark(d_b_out)

        (o0, o1, o2, o3, o4) = line(*(ors[k] for k in range(nc)))
        o_rec = jnp.concatenate([o0, o1, o2, o3, o4], axis=0)
        (o_rec, gg) = line(o_rec, G)
        late = tn(o_rec, gg)
        line.mark(late)
        late_p = lax.ppermute(late, jo, ((0, 1), (3, 2)))
        (oo, orr) = line(o_all, o_rec)
        y = (X.astype(F32) + nn(oo, wo_own) + nn(orr, wo_oth) + b_out).astype(BF16)
        line.mark(y)
        (l1, l2) = line(late, late_p)
        late = l1 + l2
        line.mark(late)
        late_y = lax.ppermute(late, ja, ((1, 5), (5, 1), (2, 6), (6, 2)))

        d_scale, d_bias, sts, dxs = [], [], [], []

        def dxa(i):
            (own, rec) = line(dh_own[i], dh_rec[i])
            dh = own + rec
            xh = (xs[i].astype(F32) - means[i]) * invs[i]
            g = dh * ln_scale
            d_scale.append(jnp.sum(dh * xh, axis=0))
            d_bias.append(jnp.sum(dh, axis=0))
            st = jnp.stack([jnp.sum(g, axis=-1), jnp.sum(g * xh, axis=-1)])
            line.mark(st)
            sts.append(st)

        def dxb(i):
            a, n = spans[i]
            (own, rec) = line(dh_own[i], dh_rec[i])
            s0 = st_all[0, a : a + n][:, None]
            s1 = st_all[1, a : a + n][:, None]
            xh = (xs[i].astype(F32) - means[i]) * invs[i]
            v = (gs[i].astype(F32) + invs[i] * ((own + rec) * ln_scale - s0 - xh * s1)).astype(BF16)
            line.mark(v)
            dxs.append(v)

        fin(0)
        fin(1)
        dxa(0)
        fin(2)
        dxa(1)
        (e, l, ey, ly) = line(early, late, early_y, late_y)
        d_w_out = jnp.where(same, e + ey, l + ly)
        line.mark(d_w_out)
        dxa(2)
        dxa(3)
        fin(3)
        dxa(4)
        st_all = jnp.concatenate(sts, axis=1)
        st_all = (st_all + over(COL, st_all)) / d_model
        for i in range(nc):
            dxb(i)
        dx = jnp.concatenate(dxs, axis=0)
        d_scale = functools.reduce(lambda p, q: p + q, d_scale)
        d_bias = functools.reduce(lambda p, q: p + q, d_bias)
        (d_b_qkv, d_b_out, d_scale, d_bias) = line(d_b_qkv, d_b_out, d_scale, d_bias)
        d_b_qkv, d_b_out, d_scale, d_bias = lax.psum((d_b_qkv, d_b_out, d_scale, d_bias), (DEP, ROW))
        line.mark(d_bias)
        fin(4)
        fin(5)
        return (y.reshape(x.shape), dx.reshape(x.shape), d_w_qkv, d_b_qkv, d_w_out, d_b_out, d_scale, d_bias)

    return jax.shard_map(
        block_fn,
        mesh=mesh,
        in_specs=(act_spec, vec_spec, vec_spec, mat_spec, head_vec_spec, mat_spec, vec_spec, act_spec),
        out_specs=(act_spec, act_spec, mat_spec, head_vec_spec, mat_spec, vec_spec, vec_spec, vec_spec),
        check_vma=False,
    )
```

time: 5500 us -> 3620 us (0.66)
  waiting for transfers between devices: 3440 us -> 1610 us
  matrix products: 1470 us -> 1120 us
  Pallas kernels: 0 us -> 311 us
  local copies, waits for them, and re-layouts: 221 us -> 118 us
  starting transfers between devices: 0.89 us -> 62 us
    ppermute x0 -> x43, waiting for transfers between devices: none -> 1610 us  [the longest x39 1610 us: over(): return lax.ppermute(v, axis, SWAP)]
    psum x1 -> x0, waiting for transfers between devices: 1380 us -> none  [block_fn(): lax.psum(lax.psum_scatter(w_qkv_part, 'row', scatter_dimension=0, tiled=T...]
    reduce_scatter x3 -> x0, waiting for transfers between devices: 1290 us -> none  [the longest x1 648 us: block_fn(): lax.psum_scatter(d_out_part, 'col', scatter_dimension=2, tiled=True)]
    all_gather x4 -> x0, waiting for transfers between devices: 762 us -> none  [the longest x1 384 us: block_fn(): h_full = lax.all_gather(h_loc, 'col', axis=2, tiled=True)]
    dot_general x12 -> x41, matrix products: 1470 us -> 1120 us  [the longest x20 404 us: nt(): lax.dot_general(a, b, (((1,), (1,)), ((), ())), preferred_element_type=F32)]
    pallas_call x0 -> x15, Pallas kernels: none -> 311 us  [the longest x5 144 us: attn_bwd(): pl.pallas_call(functools.partial(attn_bwd_kernel, hb, hd), out_shape=(jax...]
    reshape x4 -> x1, local copies, waits for them, and re-layouts: 140 us -> 0.61 us  [block_fn(): d_b_qkv = jnp.sum(dd.astype(F32), axis=0).reshape(heads, three_hd)]
    sub x2 -> x0, other arithmetic: 129 us -> none  [the longest x1 129 us: block_fn(): attn_prob = jax.nn.softmax(jnp.where(causal, scores, -1e+30), axis=-1)]
  transfers between devices with their start and end apart: 9 -> 43, of which waited for: 6 -> 13; matrix products, arithmetic and copies ran while one was open for 35% -> 39% of each run, Pallas kernels for 0% -> 8%
where the time goes in v1:
time: 3620 us; the launch traced here: 3610 us
  waiting for transfers between devices  1610 us (44%)
  matrix products  1120 us (31%)
  Pallas kernels  311 us (9%)
  other arithmetic  294 us (8%)
  local copies, waits for them, and re-layouts  118 us (3%)
  blocking collectives  84.2 us (2%)
  starting transfers between devices  62 us (2%)
    ppermute x39, waiting for transfers between devices, over(): return lax.ppermute(v, axis, SWAP)  1610 us
    dot_general x20, matrix products, nt(): lax.dot_general(a, b, (((1,), (1,)), ((), ())), preferred_element_type=F32)  404 us
    dot_general x14, matrix products, tn(): lax.dot_general(a, b, (((0,), (0,)), ((), ())), preferred_element_type=F32)  380 us
    dot_general x7, matrix products, nn(): lax.dot_general(a, b, (((1,), (0,)), ((), ())), preferred_element_type=F32)  340 us
    pallas_call x5, Pallas kernels, attn_bwd(): pl.pallas_call(functools.partial(attn_bwd_kernel, hb, hd), out_shape=(jax...  144 us
    pallas_call x5, Pallas kernels, attn_fwd(): pl.pallas_call(functools.partial(attn_fwd_kernel, hb, hd), out_shape=(jax...  118 us
    psum x1, blocking collectives, block_fn(): lax.psum((d_b_qkv, d_b_out, d_scale, d_bias), (DEP, ROW))  84.2 us
  transfers between devices with their start and end apart: 43, of which 13 were waited for; matrix products, arithmetic and copies ran while one was open for 39% of the time, Pallas kernels for 8%

profile of v1, /device:TPU:0, one launch (start us, length us, event | category | flops | bytes accessed | tf_op | source)
XLA Modules:
  0.0 3608.1 jit_solution(10714959735447622461)
XLA Ops:
  20.3 80.4 %collective-permute-done.7 = f32[4096]{0:T(1024)S(1)} collective-permute-done((f32[4096]{0:T(1024)S(1)}, f32[4096]{0:T(1024)S(1)}, u32[]{:S(2)}, u32[]{:S(2)}) %collective-permute-start.7) | collective-permute-done | bytes 16416 | tf_op jit(solution)/shard_map/ppermute | solution.py:279
  158.1 126.1 %collective-permute-done.4.xp_ref = bf16[1024,2048]{1,0:T(8,128)(2,1)S(1)} collective-permute-done((bf16[1024,2048]{1,0:T(8,128)(2,1)}, bf16[1024,2048]{1,0:T(8,128)(2,1)S(1)}, u32[]{:S(2)}, u32[]{:S(2)}) %collective-permute-start.4) | collective-permute-done | bytes 4194336 | tf_op jit(solution)/shard_map/ppermute | solution.py:279
  297.0 60.1 %add_convert_fusion.2.qkv_ref = bf16[1024,6144]{1,0:T(8,128)(2,1)} fusion(f32[6144]{0:T(1024)S(1)} %add.201, bf16[1024,4096]{1,0:T(8,128)(2,1)} %get-tuple-element.198, bf16[4096,6144]{1,0:T(8,128)(2,1)} %constant_dynamic-update-slice_fusion), kind=kOutput, calls=%fused_computation.8 | convolution fusion | flops 51552190464 | bytes 71327744 | tf_op jit(solution)/shard_map/dot_general | solution.py:28
  397.2 60.1 %add_convert_fusion.1.qkv_ref = bf16[1024,6144]{1,0:T(8,128)(2,1)} fusion(f32[6144]{0:T(1024)S(1)} %add.201, bf16[1024,4096]{1,0:T(8,128)(2,1)} %get-tuple-element.204, bf16[4096,6144]{1,0:T(8,128)(2,1)} %constant_dynamic-update-slice_fusion), kind=kOutput, calls=%fused_computation.7 | convolution fusion | flops 51552190464 | bytes 71327744 | tf_op jit(solution)/shard_map/dot_general | solution.py:28
  497.8 60.0 %add_convert_fusion.qkv_ref = bf16[1024,6144]{1,0:T(8,128)(2,1)} fusion(f32[6144]{0:T(1024)S(1)} %add.201, bf16[1024,4096]{1,0:T(8,128)(2,1)} %get-tuple-element.211, bf16[4096,6144]{1,0:T(8,128)(2,1)} %constant_dynamic-update-slice_fusion), kind=kOutput, calls=%fused_computation.6 | convolution fusion | flops 51552190464 | bytes 71327744 | tf_op jit(solution)/shard_map/dot_general | solution.py:28
  595.1 33.7 add_convert_fusion.4.qkv_ref
  652.5 33.8 add_convert_fusion.3.qkv_ref
  701.9 43.8 %fusion.70 = f32[2048,2048]{1,0:T(8,128)} fusion(bf16[4096,2048]{1,0:T(8,128)(2,1)} %get-tuple-element.326, bf16[4096,2048]{1,0:T(8,128)(2,1)} %bitcast.165), kind=kOutput, calls=%fused_computation.139 | convolution fusion | flops 34359738368 | bytes 50331648 | tf_op jit(solution)/shard_map/dot_general | solution.py:24
  779.5 77.1 %collective-permute-done.8 = bf16[1024,2048]{1,0:T(8,128)(2,1)} collective-permute-done((bf16[1024,2048]{1,0:T(8,128)(2,1)}, bf16[1024,2048]{1,0:T(8,128)(2,1)}, u32[]{:S(2)}, u32[]{:S(2)}) %collective-permute-start.8) | collective-permute-done | bytes 4194336 | tf_op jit(solution)/shard_map/ppermute | solution.py:279
  871.4 75.0 %collective-permute-done.14 = bf16[1024,2048]{1,0:T(8,128)(2,1)} collective-permute-done((bf16[1024,2048]{1,0:T(8,128)(2,1)}, bf16[1024,2048]{1,0:T(8,128)(2,1)}, u32[]{:S(2)}, u32[]{:S(2)}) %collective-permute-start.14) | collective-permute-done | bytes 4194336 | tf_op jit(solution)/shard_map/ppermute | solution.py:279
  972.9 35.3 attn_bwd.5
  1081.4 35.2 attn_bwd.6
  1116.6 35.6 attn_bwd.7
  1299.1 32.5 broadcast_select_fusion
  1380.4 34.7 fusion.13
  1464.4 34.7 fusion.11
  1547.8 34.9 fusion.9
  1700.8 34.8 fusion.7
  1735.5 34.6 fusion.5
  1770.1 34.9 fusion.3
  1869.6 56.1 %collective-permute-done.20 = bf16[512,2048]{1,0:T(8,128)(2,1)} collective-permute-done((bf16[512,2048]{1,0:T(8,128)(2,1)}, bf16[512,2048]{1,0:T(8,128)(2,1)}, u32[]{:S(2)}, u32[]{:S(2)}) %collective-permute-start.20) | collective-permute-done | bytes 2097184 | tf_op jit(solution)/shard_map/ppermute | solution.py:279
  1925.8 44.0 %collective-permute-done.21 = bf16[512,2048]{1,0:T(8,128)(2,1)} collective-permute-done((bf16[512,2048]{1,0:T(8,128)(2,1)}, bf16[512,2048]{1,0:T(8,128)(2,1)}, u32[]{:S(2)}, u32[]{:S(2)}) %collective-permute-start.21) | collective-permute-done | bytes 2097184 | tf_op jit(solution)/shard_map/ppermute | solution.py:279
  1990.5 43.8 %fusion.76 = f32[2048,2048]{1,0:T(8,128)} fusion(bf16[4096,2048]{1,0:T(8,128)(2,1)} %constant_dynamic-update-slice_fusion.2, bf16[4096,2048]{1,0:T(8,128)(2,1)} %bitcast.167), kind=kOutput, calls=%fused_computation.145 | convolution fusion | flops 34359738368 | bytes 50331648 | tf_op jit(solution)/shard_map/dot_general | solution.py:24
  2044.9 43.6 %fusion.77 = f32[4096,2048]{1,0:T(8,128)} fusion(bf16[4096,2048]{1,0:T(8,128)(2,1)} %get-tuple-element.326, bf16[2048,2048]{1,0:T(8,128)(2,1)} %get-tuple-element.425), kind=kOutput, calls=%fused_computation.146 | convolution fusion | flops 34359738368 | bytes 58720256 | tf_op jit(solution)/shard_map/dot_general | solution.py:28
  2088.4 48.6 %fusion.2 = bf16[4096,2048]{1,0:T(8,128)(2,1)} fusion(f32[4096,2048]{1,0:T(8,128)} %fusion.77, bf16[8,512,2048]{2,1,0:T(8,128)(2,1)} %param.8, f32[2048]{0:T(1024)S(1)} %copy-done.24, bf16[4096,2048]{1,0:T(8,128)(2,1)} %constant_dynamic-update-slice_fusion.2, bf16[2048,2048]{1,0:T(8,128)(2,1)} %copy-done.15), kind=kOutput, calls=%fused_computation.4 | convolution fusion | flops 34401681408 | bytes 92282880 | tf_op jit(solution)/shard_map/dot_general | solution.py:28
  2158.1 66.9 %collective-permute-done.39 = f32[2048,1024]{1,0:T(8,128)} collective-permute-done((f32[2048,1024]{1,0:T(8,128)}, f32[2048,1024]{1,0:T(8,128)}, u32[]{:S(2)}, u32[]{:S(2)}) %collective-permute-start.39) | collective-permute-done | bytes 8388640 | tf_op jit(solution)/shard_map/ppermute | solution.py:279
  2231.4 173.4 %collective-permute-done.38 = f32[2048,1024]{1,0:T(8,128)} collective-permute-done((f32[2048,1024]{1,0:T(8,128)}, f32[2048,1024]{1,0:T(8,128)}, u32[]{:S(2)}, u32[]{:S(2)}) %collective-permute-start.38) | collective-permute-done | bytes 8388640 | tf_op jit(solution)/shard_map/ppermute | solution.py:279
  2406.2 178.3 %collective-permute-done.37 = f32[2048,1024]{1,0:T(8,128)} collective-permute-done((f32[2048,1024]{1,0:T(8,128)}, f32[2048,1024]{1,0:T(8,128)}, u32[]{:S(2)}, u32[]{:S(2)}) %collective-permute-start.37) | collective-permute-done | bytes 8388640 | tf_op jit(solution)/shard_map/ppermute | solution.py:279
  2584.6 531.7 %collective-permute-done.30 = f32[2048,1024]{1,0:T(8,128)S(1)} collective-permute-done((f32[2048,1024]{1,0:T(8,128)S(1)}, f32[2048,1024]{1,0:T(8,128)S(1)}, u32[]{:S(2)}, u32[]{:S(2)}) %collective-permute-start.30) | collective-permute-done | bytes 8388640 | tf_op jit(solution)/shard_map/ppermute | solution.py:279
  3195.6 197.0 %collective-permute-done.29 = f32[512,2048]{1,0:T(8,128)} collective-permute-done((f32[512,2048]{1,0:T(8,128)}, f32[512,2048]{1,0:T(8,128)}, u32[]{:S(2)}, u32[]{:S(2)}) %collective-permute-start.29) | collective-permute-done | bytes 4194336 | tf_op jit(solution)/shard_map/ppermute | solution.py:279
  3403.0 29.3 add_select_fusion
  3499.1 84.2 %all-reduce.1 = (f32[2048]{0:T(1024)}, f32[16,384]{1,0:T(8,128)}, f32[2048]{0:T(1024)}, f32[2048]{0:T(1024)}) all-reduce(f32[2048]{0:T(1024)S(1)} %get-tuple-element.372, f32[16,384]{1,0:T(8,128)S(1)} %copy-done.20, f32[2048]{0:T(1024)S(1)} %copy-done.21, ...), channel_id=1, replica_groups=mesh['depth'=2,'col'=2,'row'=2] {'depth','row'}, use_global_device_ids=true, to_apply=%region_22.23 | all-reduce | flops 12288 | bytes 98304 | tf_op jit(solution)/shard_map/psum | solution.py:483
  (233 shorter events, 1112.7 us)
Async XLA Ops:
  0.7 112.8 %collective-permute-start.5 = (bf16[2048,6144]{1,0:T(8,128)(2,1)}, bf16[2048,6144]{1,0:T(8,128)(2,1)}, u32[]{:S(2)}, u32[]{:S(2)}) collective-permute-start(bf16[2048,6144]{1,0:T(8,128)(2,1)} %param.11), channel_id=1, source_target_pairs={{0,1},{1,0},{2,3},{3,2},{4,5},{5,4},{6,7},{7,6}} | collective-permute-start | bytes 75497480 | tf_op jit(solution)/shard_map/ppermute | solution.py:279
  1.5 100.9 %collective-permute-start.6 = (bf16[2048,2048]{1,0:T(8,128)(2,1)}, bf16[2048,2048]{1,0:T(8,128)(2,1)}, u32[]{:S(2)}, u32[]{:S(2)}) collective-permute-start(bf16[2048,2048]{1,0:T(8,128)(2,1)} %param.13), channel_id=1, source_target_pairs={{0,1},{1,0},{2,3},{3,2},{4,5},{5,4},{6,7},{7,6}} | collective-permute-start | bytes 25165832 | tf_op jit(solution)/shard_map/ppermute | solution.py:279
  6.3 638.1 %collective-permute-start = (bf16[512,2048]{1,0:T(8,128)(2,1)}, bf16[512,2048]{1,0:T(8,128)(2,1)}, u32[]{:S(2)}, u32[]{:S(2)}) collective-permute-start(bf16[512,2048]{1,0:T(8,128)(2,1)} %get-tuple-element.221.xo_ref), channel_id=1, source_target_pairs={{0,2},{2,0},{1,3},{3,1},{4,6},{6,4},{5,7},{7,5}} | collective-permute-start | bytes 6291464 | tf_op jit(solution)/shard_map/ppermute | solution.py:279
  9.3 577.6 %collective-permute-start.1 = (bf16[512,2048]{1,0:T(8,128)(2,1)}, bf16[512,2048]{1,0:T(8,128)(2,1)}, u32[]{:S(2)}, u32[]{:S(2)}) collective-permute-start(bf16[512,2048]{1,0:T(8,128)(2,1)} %get-tuple-element.214.xo_ref), channel_id=1, source_target_pairs={{0,2},{2,0},{1,3},{3,1},{4,6},{6,4},{5,7},{7,5}} | collective-permute-start | bytes 6291464 | tf_op jit(solution)/shard_map/ppermute | solution.py:279
  100.6 385.8 %collective-permute-start.2 = (bf16[1024,2048]{1,0:T(8,128)(2,1)}, bf16[1024,2048]{1,0:T(8,128)(2,1)}, u32[]{:S(2)}, u32[]{:S(2)}) collective-permute-start(bf16[1024,2048]{1,0:T(8,128)(2,1)} %bitcast.137), channel_id=1, source_target_pairs={{0,2},{2,0},{1,3},{3,1},{4,6},{6,4},{5,7},{7,5}} | collective-permute-start | bytes 12582920 | tf_op jit(solution)/shard_map/ppermute | solution.py:279
  102.4 181.8 %collective-permute-start.4 = (bf16[1024,2048]{1,0:T(8,128)(2,1)}, bf16[1024,2048]{1,0:T(8,128)(2,1)S(1)}, u32[]{:S(2)}, u32[]{:S(2)}) collective-permute-start(bf16[1024,2048]{1,0:T(8,128)(2,1)} %bitcast.141), channel_id=1, source_target_pairs={{0,2},{2,0},{1,3},{3,1},{4,6},{6,4},{5,7},{7,5}} | collective-permute-start | bytes 12582920 | tf_op jit(solution)/shard_map/ppermute | solution.py:279
  113.4 272.6 %collective-permute-start.3 = (bf16[1024,2048]{1,0:T(8,128)(2,1)S(1)}, bf16[1024,2048]{1,0:T(8,128)(2,1)}, u32[]{:S(2)}, u32[]{:S(2)}) collective-permute-start(bf16[1024,2048]{1,0:T(8,128)(2,1)S(1)} %bitcast.139), channel_id=1, source_target_pairs={{0,2},{2,0},{1,3},{3,1},{4,6},{6,4},{5,7},{7,5}} | collective-permute-start | bytes 12582920 | tf_op jit(solution)/shard_map/ppermute | solution.py:279
  284.2 417.7 %collective-permute-start.9 = (bf16[512,2048]{1,0:T(8,128)(2,1)}, bf16[512,2048]{1,0:T(8,128)(2,1)}, u32[]{:S(2)}, u32[]{:S(2)}) collective-permute-start(bf16[512,2048]{1,0:T(8,128)(2,1)} %constant_dynamic-slice_fusion), channel_id=1, source_target_pairs={{0,2},{2,0},{1,3},{3,1},{4,6},{6,4},{5,7},{7,5}} | collective-permute-start | bytes 6291464 | tf_op jit(solution)/shard_map/ppermute | solution.py:279
  745.7 290.7 %collective-permute-start.13 = (f32[2048,2048]{1,0:T(8,128)}, f32[2048,2048]{1,0:T(8,128)}, u32[]{:S(2)}, u32[]{:S(2)}) collective-permute-start(f32[2048,2048]{1,0:T(8,128)} %fusion.70), channel_id=1, source_target_pairs={{1,0},{2,3},{5,4},{6,7}} | collective-permute-start | bytes 50331656 | tf_op jit(solution)/shard_map/ppermute | solution.py:329
  772.4 174.0 %collective-permute-start.14 = (bf16[1024,2048]{1,0:T(8,128)(2,1)}, bf16[1024,2048]{1,0:T(8,128)(2,1)}, u32[]{:S(2)}, u32[]{:S(2)}) collective-permute-start(bf16[1024,2048]{1,0:T(8,128)(2,1)} %bitcast.14), channel_id=1, source_target_pairs={{0,2},{2,0},{1,3},{3,1},{4,6},{6,4},{5,7},{7,5}} | collective-permute-start | bytes 12582920 | tf_op jit(solution)/shard_map/ppermute | solution.py:279
  777.4 276.4 %collective-permute-start.12 = (bf16[1024,2048]{1,0:T(8,128)(2,1)S(1)}, bf16[1024,2048]{1,0:T(8,128)(2,1)}, u32[]{:S(2)}, u32[]{:S(2)}) collective-permute-start(bf16[1024,2048]{1,0:T(8,128)(2,1)S(1)} %bitcast.168), channel_id=1, source_target_pairs={{0,2},{2,0},{1,3},{3,1},{4,6},{6,4},{5,7},{7,5}} | collective-permute-start | bytes 12582920 | tf_op jit(solution)/shard_map/ppermute | solution.py:279
  856.5 295.6 %collective-permute-start.17 = (bf16[512,2048]{1,0:T(8,128)(2,1)}, bf16[512,2048]{1,0:T(8,128)(2,1)}, u32[]{:S(2)}, u32[]{:S(2)}) collective-permute-start(bf16[512,2048]{1,0:T(8,128)(2,1)} %get-tuple-element.250), channel_id=1, source_target_pairs={{0,2},{2,0},{1,3},{3,1},{4,6},{6,4},{5,7},{7,5}} | collective-permute-start | bytes 6291464 | tf_op jit(solution)/shard_map/ppermute | solution.py:279
  862.0 325.6 %collective-permute-start.19 = (bf16[512,2048]{1,0:T(8,128)(2,1)}, bf16[512,2048]{1,0:T(8,128)(2,1)}, u32[]{:S(2)}, u32[]{:S(2)}) collective-permute-start(bf16[512,2048]{1,0:T(8,128)(2,1)} %get-tuple-element.256), channel_id=1, source_target_pairs={{0,2},{2,0},{1,3},{3,1},{4,6},{6,4},{5,7},{7,5}} | collective-permute-start | bytes 6291464 | tf_op jit(solution)/shard_map/ppermute | solution.py:279
  1607.3 362.5 %collective-permute-start.15 = (bf16[1024,2048]{1,0:T(8,128)(2,1)}, bf16[1024,2048]{1,0:T(8,128)(2,1)}, u32[]{:S(2)}, u32[]{:S(2)}) collective-permute-start(bf16[1024,2048]{1,0:T(8,128)(2,1)} %get-tuple-element.247), channel_id=1, source_target_pairs={{0,2},{2,0},{1,3},{3,1},{4,6},{6,4},{5,7},{7,5}} | collective-permute-start | bytes 12582920 | tf_op jit(solution)/shard_map/ppermute | solution.py:279
  1608.7 361.1 %collective-permute-start.16 = (bf16[1024,2048]{1,0:T(8,128)(2,1)}, bf16[1024,2048]{1,0:T(8,128)(2,1)}, u32[]{:S(2)}, u32[]{:S(2)}) collective-permute-start(bf16[1024,2048]{1,0:T(8,128)(2,1)} %get-tuple-element.248), channel_id=1, source_target_pairs={{0,2},{2,0},{1,3},{3,1},{4,6},{6,4},{5,7},{7,5}} | collective-permute-start | bytes 12582920 | tf_op jit(solution)/shard_map/ppermute | solution.py:279
  1609.3 360.4 %collective-permute-start.18 = (bf16[1024,2048]{1,0:T(8,128)(2,1)}, bf16[1024,2048]{1,0:T(8,128)(2,1)}, u32[]{:S(2)}, u32[]{:S(2)}) collective-permute-start(bf16[1024,2048]{1,0:T(8,128)(2,1)} %get-tuple-element.254), channel_id=1, source_target_pairs={{0,2},{2,0},{1,3},{3,1},{4,6},{6,4},{5,7},{7,5}} | collective-permute-start | bytes 12582920 | tf_op jit(solution)/shard_map/ppermute | solution.py:279
  1610.7 315.0 %collective-permute-start.20 = (bf16[512,2048]{1,0:T(8,128)(2,1)}, bf16[512,2048]{1,0:T(8,128)(2,1)}, u32[]{:S(2)}, u32[]{:S(2)}) collective-permute-start(bf16[512,2048]{1,0:T(8,128)(2,1)} %get-tuple-element.260), channel_id=1, source_target_pairs={{0,2},{2,0},{1,3},{3,1},{4,6},{6,4},{5,7},{7,5}} | collective-permute-start | bytes 6291464 | tf_op jit(solution)/shard_map/ppermute | solution.py:279
  1655.8 314.0 %collective-permute-start.21 = (bf16[512,2048]{1,0:T(8,128)(2,1)}, bf16[512,2048]{1,0:T(8,128)(2,1)}, u32[]{:S(2)}, u32[]{:S(2)}) collective-permute-start(bf16[512,2048]{1,0:T(8,128)(2,1)} %get-tuple-element.261), channel_id=1, source_target_pairs={{0,2},{2,0},{1,3},{3,1},{4,6},{6,4},{5,7},{7,5}} | collective-permute-start | bytes 6291464 | tf_op jit(solution)/shard_map/ppermute | solution.py:279
  2034.2 102.8 %collective-permute-start.33 = (f32[2048,2048]{1,0:T(8,128)}, f32[2048,2048]{1,0:T(8,128)}, u32[]{:S(2)}, u32[]{:S(2)}) collective-permute-start(f32[2048,2048]{1,0:T(8,128)} %fusion.76), channel_id=1, source_target_pairs={{0,1},{3,2},{4,5},{7,6}} | collective-permute-start | bytes 50331656 | tf_op jit(solution)/shard_map/ppermute | solution.py:431
  2041.4 183.6 %collective-permute-start.39 = (f32[2048,1024]{1,0:T(8,128)}, f32[2048,1024]{1,0:T(8,128)}, u32[]{:S(2)}, u32[]{:S(2)}) collective-permute-start(f32[2048,1024]{1,0:T(8,128)} %fusion.47), channel_id=1, source_target_pairs={{0,4},{4,0},{1,5},{5,1},{2,6},{6,2},{3,7},{7,3}} | collective-permute-start | bytes 25165832 | tf_op jit(solution)/shard_map/ppermute | solution.py:279
  2042.8 362.0 %collective-permute-start.38 = (f32[2048,1024]{1,0:T(8,128)}, f32[2048,1024]{1,0:T(8,128)}, u32[]{:S(2)}, u32[]{:S(2)}) collective-permute-start(f32[2048,1024]{1,0:T(8,128)} %fusion.50), channel_id=1, source_target_pairs={{0,4},{4,0},{1,5},{5,1},{2,6},{6,2},{3,7},{7,3}} | collective-permute-start | bytes 25165832 | tf_op jit(solution)/shard_map/ppermute | solution.py:279
  2043.4 362.8 %collective-permute-start.28 = (f32[1024,2048]{1,0:T(8,128)}, f32[1024,2048]{1,0:T(8,128)}, u32[]{:S(2)}, u32[]{:S(2)}) collective-permute-start(f32[1024,2048]{1,0:T(8,128)} %fusion.13), channel_id=1, source_target_pairs={{0,2},{2,0},{1,3},{3,1},{4,6},{6,4},{5,7},{7,5}} | collective-permute-start | bytes 25165832 | tf_op jit(solution)/shard_map/ppermute | solution.py:279
  2043.4 541.1 %collective-permute-start.37 = (f32[2048,1024]{1,0:T(8,128)}, f32[2048,1024]{1,0:T(8,128)}, u32[]{:S(2)}, u32[]{:S(2)}) collective-permute-start(f32[2048,1024]{1,0:T(8,128)} %fusion.53), channel_id=1, source_target_pairs={{0,4},{4,0},{1,5},{5,1},{2,6},{6,2},{3,7},{7,3}} | collective-permute-start | bytes 25165832 | tf_op jit(solution)/shard_map/ppermute | solution.py:279
  2137.0 1266.0 %collective-permute-start.34 = (f32[2048,2048]{1,0:T(8,128)}, f32[2048,2048]{1,0:T(8,128)}, u32[]{:S(2)}, u32[]{:S(2)}) collective-permute-start(f32[2048,2048]{1,0:T(8,128)} %add.212), channel_id=1, source_target_pairs={{0,4},{4,0},{3,7},{7,3}} | collective-permute-start | bytes 50331656 | tf_op jit(solution)/shard_map/ppermute | solution.py:348
  2225.0 1177.9 %collective-permute-start.35 = (f32[2048,2048]{1,0:T(8,128)}, f32[2048,2048]{1,0:T(8,128)}, u32[]{:S(2)}, u32[]{:S(2)}) collective-permute-start(f32[2048,2048]{1,0:T(8,128)} %add.227), channel_id=1, source_target_pairs={{1,5},{5,1},{2,6},{6,2}} | collective-permute-start | bytes 50331656 | tf_op jit(solution)/shard_map/ppermute | solution.py:438
  2404.8 711.4 %collective-permute-start.30 = (f32[2048,1024]{1,0:T(8,128)S(1)}, f32[2048,1024]{1,0:T(8,128)S(1)}, u32[]{:S(2)}, u32[]{:S(2)}) collective-permute-start(f32[2048,1024]{1,0:T(8,128)S(1)} %copy-done.16), channel_id=1, source_target_pairs={{0,4},{4,0},{1,5},{5,1},{2,6},{6,2},{3,7},{7,3}} | collective-permute-start | bytes 25165832 | tf_op jit(solution)/shard_map/ppermute | solution.py:279
  2406.2 775.8 %collective-permute-start.36 = (f32[1024,2048]{1,0:T(8,128)}, f32[1024,2048]{1,0:T(8,128)}, u32[]{:S(2)}, u32[]{:S(2)}) collective-permute-start(f32[1024,2048]{1,0:T(8,128)} %fusion.11), channel_id=1, source_target_pairs={{0,2},{2,0},{1,3},{3,1},{4,6},{6,4},{5,7},{7,5}} | collective-permute-start | bytes 25165832 | tf_op jit(solution)/shard_map/ppermute | solution.py:279
  2584.6 535.0 %collective-permute-start.31 = (f32[512,2048]{1,0:T(8,128)S(1)}, f32[512,2048]{1,0:T(8,128)}, u32[]{:S(2)}, u32[]{:S(2)}) collective-permute-start(f32[512,2048]{1,0:T(8,128)S(1)} %copy-done.23), channel_id=1, source_target_pairs={{0,2},{2,0},{1,3},{3,1},{4,6},{6,4},{5,7},{7,5}} | collective-permute-start | bytes 12582920 | tf_op jit(solution)/shard_map/ppermute | solution.py:279
  3119.6 312.7 %collective-permute-start.32 = (f32[1024,2048]{1,0:T(8,128)}, f32[1024,2048]{1,0:T(8,128)}, u32[]{:S(2)}, u32[]{:S(2)}) collective-permute-start(f32[1024,2048]{1,0:T(8,128)} %fusion.9), channel_id=1, source_target_pairs={{0,2},{2,0},{1,3},{3,1},{4,6},{6,4},{5,7},{7,5}} | collective-permute-start | bytes 25165832 | tf_op jit(solution)/shard_map/ppermute | solution.py:279
  3119.6 273.1 %collective-permute-start.29 = (f32[512,2048]{1,0:T(8,128)}, f32[512,2048]{1,0:T(8,128)}, u32[]{:S(2)}, u32[]{:S(2)}) collective-permute-start(f32[512,2048]{1,0:T(8,128)} %fusion.43), channel_id=1, source_target_pairs={{0,2},{2,0},{1,3},{3,1},{4,6},{6,4},{5,7},{7,5}} | collective-permute-start | bytes 12582920 | tf_op jit(solution)/shard_map/ppermute | solution.py:279
  3182.1 401.2 %collective-permute-start.41 = (f32[2048,1024]{1,0:T(8,128)}, f32[2048,1024]{1,0:T(8,128)}, u32[]{:S(2)}, u32[]{:S(2)}) collective-permute-start(f32[2048,1024]{1,0:T(8,128)} %fusion.59), channel_id=1, source_target_pairs={{0,4},{4,0},{1,5},{5,1},{2,6},{6,2},{3,7},{7,3}} | collective-permute-start | bytes 25165832 | tf_op jit(solution)/shard_map/ppermute | solution.py:279
  3392.6 202.8 %collective-permute-start.42 = (f32[2048,1024]{1,0:T(8,128)}, f32[2048,1024]{1,0:T(8,128)}, u32[]{:S(2)}, u32[]{:S(2)}) collective-permute-start(f32[2048,1024]{1,0:T(8,128)} %fusion.62), channel_id=1, source_target_pairs={{0,4},{4,0},{1,5},{5,1},{2,6},{6,2},{3,7},{7,3}} | collective-permute-start | bytes 25165832 | tf_op jit(solution)/shard_map/ppermute | solution.py:279
  (42 other events, 2249.1 us)
